TPU v7x, 32 devices: a whole 2x2x4 slice. The times are simulated.
32 devices in a mesh: blk: 8 (over z, y), rep: 4 (over x, core).
Axes of the slice: x: 2, y: 2, z: 4, core: 2. Of those that a mesh axis runs over, the one named last changes fastest.
Arguments:
- tokens: bfloat16 [4096, 8192], P(('blk', 'rep')), may hold values from -6 to 6
- gate_weight: bfloat16 [8, 8192], P('blk'), may hold values from -0.0625 to 0.0625
- up_weight: bfloat16 [8, 8192], P('blk'), may hold values from -0.0625 to 0.0625
- down_weight: bfloat16 [8, 8192], P('blk'), may hold values from -2 to 2
Outputs:
- grad_gate: float32 [8, 8192], P('blk')
- grad_up: float32 [8, 8192], P('blk')
- grad_down: float32 [8, 8192], P('blk')
All inputs are finite; a program needn't handle non-finite values.
Results may differ from a plain program's by a relative error of at most 0.0027.
Values may be sent and summed in bfloat16 or wider, within the bound.
A program may use at most 64 MiB of HBM per device.

v0:
```python
import jax
import jax.numpy as jnp
from jax import lax
from jax.sharding import PartitionSpec as P


def per_device(tokens, gate_weight, up_weight, down_weight):
    tok_rows = tokens.shape[0]
    features = tokens.shape[1]
    cycle_size = lax.axis_size("blk")
    group_size = lax.axis_size("rep")
    loss_scale = float(tok_rows * cycle_size * group_size) ** (-0.5)
    right_numbers = (((1,), (1,)), ((), ()))
    left_numbers = (((0,), (0,)), ((), ()))
    gate_piece = lax.all_gather(gate_weight, "blk", axis=0, tiled=True)
    up_piece = lax.all_gather(up_weight, "blk", axis=0, tiled=True)
    down_piece = lax.all_gather(down_weight, "blk", axis=0, tiled=True)
    gate_pre = lax.dot_general(
        tokens, gate_piece, right_numbers, preferred_element_type=jnp.float32
    )
    up_pre = lax.dot_general(tokens, up_piece, right_numbers, preferred_element_type=jnp.float32)
    hidden_piece = (gate_pre * jax.nn.sigmoid(gate_pre) * up_pre).astype(jnp.bfloat16)
    layer_out = jnp.dot(hidden_piece, down_piece, preferred_element_type=jnp.float32)
    gate_all = gate_pre
    up_all = up_pre
    gate_full = gate_piece
    up_full = up_piece
    down_full = down_piece
    carry = (layer_out, gate_all, up_all, hidden_piece, gate_full, up_full, down_full)
    layer_out, gate_pre, up_pre, hidden, gate_full, up_full, down_full = carry
    cotangent = (layer_out * loss_scale).astype(jnp.bfloat16)
    hidden_grad = lax.dot_general(
        cotangent, down_full, right_numbers, preferred_element_type=jnp.float32
    )
    sigmoid_gate = jax.nn.sigmoid(gate_pre)
    active = gate_pre * sigmoid_gate
    gate_grad = (
        hidden_grad * up_pre * (sigmoid_gate * (1.0 + gate_pre * (1.0 - sigmoid_gate)))
    ).astype(jnp.bfloat16)
    up_grad = (hidden_grad * active).astype(jnp.bfloat16)
    gate_term = lax.dot_general(gate_grad, tokens, left_numbers, preferred_element_type=jnp.float32)
    up_term = lax.dot_general(up_grad, tokens, left_numbers, preferred_element_type=jnp.float32)
    down_term = lax.dot_general(hidden, cotangent, left_numbers, preferred_element_type=jnp.float32)
    shares = lax.psum_scatter(
        jnp.concatenate([gate_term, up_term, down_term], axis=1),
        "blk",
        scatter_dimension=0,
        tiled=True,
    )
    totals = lax.psum(shares, "rep")
    return (totals[:, :features], totals[:, features : 2 * features], totals[:, 2 * features :])


def solution(mesh):
    in_specs = (P(("blk", "rep"), None), P("blk", None), P("blk", None), P("blk", None))
    out_specs = (P("blk", None), P("blk", None), P("blk", None))
    return jax.shard_map(
        per_device, mesh=mesh, in_specs=in_specs, out_specs=out_specs, check_vma=False
    )
```

profile of v0, /device:TPU:0, one launch (start us, length us, event | category | flops | bytes accessed | tf_op | source)
XLA Modules:
  0.0 225.2 jit_solution(10801026277273655064)
XLA Ops:
  7.2 0.0 copy-start
  7.2 0.0 all-reduce.6.cloned.1.call-start
  7.2 32.9 %all-gather.2 = bf16[8,1,8192]{2,1,0:T(2,128)(2,1)S(1)} all-gather(bf16[1,1,8192]{2,1,0:T(2,128)(2,1)} %bitcast.25), channel_id=1, replica_groups=mesh['blk'=8,'rep'=4] {'blk'}, dimensions={0}, use_global_device_ids=true | all-gather | bytes 147456 | tf_op jit(solution)/shard_map/all_gather | solution.py:17
  40.1 30.9 %all-gather = bf16[8,1,8192]{2,1,0:T(2,128)(2,1)S(1)} all-gather(bf16[1,1,8192]{2,1,0:T(2,128)(2,1)} %bitcast.26), channel_id=1, replica_groups=mesh['blk'=8,'rep'=4] {'blk'}, dimensions={0}, use_global_device_ids=true | all-gather | bytes 147456 | tf_op jit(solution)/shard_map/all_gather | solution.py:15
  71.1 30.9 %all-gather.1 = bf16[8,1,8192]{2,1,0:T(2,128)(2,1)S(1)} all-gather(bf16[1,1,8192]{2,1,0:T(2,128)(2,1)} %bitcast.27), channel_id=1, replica_groups=mesh['blk'=8,'rep'=4] {'blk'}, dimensions={0}, use_global_device_ids=true | all-gather | bytes 147456 | tf_op jit(solution)/shard_map/all_gather | solution.py:16
  102.0 0.0 copy-done
  102.0 0.7 fusion.7
  102.7 0.7 multiply_convert_fusion.2
  103.4 0.8 fusion
  104.1 0.6 fusion.1
  104.8 0.4 fusion.20
  105.2 0.4 fusion.14
  105.6 0.0 copy-start.1
  105.6 0.4 fusion.13
  106.0 1.0 pad_maximum_fusion
  106.9 0.0 all-reduce.6.cloned.1.call-update
  107.0 0.0 all-reduce.4.cloned.1.call-start
  107.0 0.0 copy-done.1
  107.0 0.6 dynamic-slice
  107.6 75.8 %all-reduce.6.cloned.1.call-done = f32[8,24576]{1,0:T(8,128)} async-done(((f32[8,24576]{1,0:T(8,128)}), f32[8,24576]{1,0:T(8,128)}) %all-reduce.6.cloned.1.call-update) | async-done | bytes 786448
  183.4 2.5 %constant_dynamic-slice_fusion = f32[1,24576]{1,0:T(1,128)} fusion(f32[8,24576]{1,0:T(8,128)} %all-reduce.6.cloned.1.call-done, u32[]{:T(128)} %bitcast.3), kind=kLoop, calls=%fused_computation.22 | loop fusion | bytes 196612
  185.9 0.0 all-reduce.4.cloned.1.call-update
  185.9 31.0 %all-reduce.4.cloned.1.call-done = f32[1,24576]{1,0:T(1,128)} async-done(((f32[1,24576]{1,0:T(1,128)}), f32[1,24576]{1,0:T(1,128)}) %all-reduce.4.cloned.1.call-update) | async-done | bytes 98320 | tf_op jit(solution)/shard_map/psum | solution.py:50
  216.9 1.4 fusion.19
Async XLA Ops:
  7.2 94.9 %copy-start = (bf16[128,8192]{1,0:T(8,128)(2,1)S(1)}, bf16[128,8192]{1,0:T(8,128)(2,1)}, u32[]{:S(2)}) copy-start(bf16[128,8192]{1,0:T(8,128)(2,1)} %param.4) | copy-start | bytes 6291460
  7.2 176.2 %all-reduce.6.cloned.1.call-start = ((), (), s32[]{:S(2)}) async-start(), calls=%async_computation.1 | async-start | bytes 1572864
  105.6 1.4 copy-start.1
  107.0 109.9 %all-reduce.4.cloned.1.call-start = ((), (), s32[]{:S(2)}) async-start(), calls=%async_computation | async-start | bytes 196608 | tf_op jit(solution)/shard_map/psum | solution.py:50
Sparse Core Ops, SparseCore 0:
  107.1 76.2 all-reduce.5
  186.0 30.8 all-reduce.3
where the time goes:
time: 225 us
  waiting for transfers between devices  107 us (48%)
  blocking collectives  94.8 us (42%)
  between operations  14.1 us (6%)
  local copies, waits for them, and re-layouts  4.51 us (2%)
  matrix products  3.94 us (2%)
    unnamed x3, waiting for transfers between devices  75.8 us
    all_gather x1, blocking collectives, per_device(): down_piece = lax.all_gather(down_weight, 'blk', axis=0, tiled=True)  32.9 us
    psum x1, waiting for transfers between devices, per_device(): totals = lax.psum(shares, 'rep')  31 us
    all_gather x1, blocking collectives, per_device(): gate_piece = lax.all_gather(gate_weight, 'blk', axis=0, tiled=True)  30.9 us
    all_gather x1, blocking collectives, per_device(): up_piece = lax.all_gather(up_weight, 'blk', axis=0, tiled=True)  30.9 us
  transfers between devices with their start and end apart: 2, of which 2 were waited for; matrix products, arithmetic and copies ran while one was open for 0% of the time, Pallas kernels for 0%

commit v1 on v0

v1 whole, which is shorter than its diff:
```python
import functools
import math

import jax
import jax.numpy as jnp
from jax import lax
from jax.experimental import pallas as pl
from jax.experimental.pallas import tpu as pltpu
from jax.sharding import PartitionSpec as P

F32, BF16 = jnp.float32, jnp.bfloat16
NT = (((1,), (1,)), ((), ()))
EXACT = lax.Precision.HIGHEST


def each(count, body):
    if count <= 32:
        for i in range(count):
            body(i)
    else:
        lax.fori_loop(0, count, lambda i, c: (body(i), c)[1], 0)


def kernel(
    B, R, PX, loss_scale,
    tok_hbm, gate_ref, up_ref, down_ref,
    out_gate, out_up, out_down,
    tok, rows_in, down_in, w_all, wd_all, gram, pair, partner_in, part, mine, send, recv, share,
    tok_sem, w_send, w_recv, d_send, d_recv, g_send, g_recv, p_send, p_recv, r_send, r_recv, o_send, o_recv,
):
    T, F = tok.shape
    XN = R // 2
    HW = F // 2
    PW = HW // PX
    me_b, me_r = lax.axis_index("blk"), lax.axis_index("rep")
    core, xi = lax.rem(me_r, 2), lax.div(me_r, 2)
    everyone = PX == XN

    def if_owner(body):
        if everyone:
            body()
        else:
            pl.when(xi < PX)(body)

    def remote(src, dst, ss, rs, b, r):
        return pltpu.make_async_remote_copy(
            src_ref=src, dst_ref=dst, send_sem=ss, recv_sem=rs,
            device_id={"blk": b, "rep": r}, device_id_type=pl.DeviceIdType.MESH,
        )

    load = pltpu.make_async_copy(tok_hbm, tok, tok_sem)
    load.start()

    barrier = pltpu.get_barrier_semaphore()

    def greet(b, r):
        pl.semaphore_signal(
            barrier, inc=1, device_id={"blk": b, "rep": r}, device_id_type=pl.DeviceIdType.MESH
        )

    def same_core(i):
        k = i + 1
        return lax.rem(me_b + k // XN, B), 2 * lax.rem(xi + k % XN, XN) + core

    each(B * XN - 1, lambda i: greet(*same_core(i)))
    each(XN, lambda i: greet(me_b, 2 * i + 1 - core))
    pl.semaphore_wait(barrier, B * XN - 1 + XN)

    my_col = pl.multiple_of(core * HW + lax.rem(xi, PX) * PW, 128)

    def d_copy(i):
        b = lax.rem(me_b + i + 1, B)
        return remote(
            down_ref.at[:, pl.ds(my_col, PW)], down_in.at[me_b], d_send.at[b], d_recv.at[me_b], b, me_r
        )

    def w_copy(which, ref, i):
        b = lax.rem(me_b + i + 1, B)
        return remote(ref, rows_in.at[which, me_b], w_send.at[which, b], w_recv.at[which, me_b], b, me_r)

    each(B - 1, lambda i: d_copy(i).start())
    each(B - 1, lambda i: (w_copy(0, gate_ref, i).start(), w_copy(1, up_ref, i).start()))

    down_in[me_b] = down_ref[:, pl.ds(my_col, PW)]
    rows_in[0, me_b] = gate_ref[...]
    rows_in[1, me_b] = up_ref[...]

    def d_arrived(i):
        b = lax.rem(me_b + i + 1, B)
        remote(down_in.at[b], down_in.at[b], d_send.at[b], d_recv.at[b], b, me_r).wait_recv()

    each(B - 1, d_arrived)
    for b in range(B):
        wd_all[b : b + 1, :] = down_in[b].astype(F32)

    def g_copy(i):
        r = lax.rem(me_r + i + 1, R)
        return remote(gram.at[me_r], gram.at[me_r], g_send.at[r], g_recv.at[me_r], me_b, r)

    def make_gram():
        wd = wd_all[...].astype(BF16)
        gram[me_r, :, :] = jnp.zeros(gram.shape[1:], F32)
        gram[me_r, :, 0:B] = lax.dot_general(wd, wd, NT, preferred_element_type=F32)
        each(R - 1, lambda i: g_copy(i).start())

    if_owner(make_gram)

    def w_arrived(i):
        b = lax.rem(me_b + i + 1, B)
        for which in range(2):
            slot = rows_in.at[which, b]
            remote(slot, slot, w_send.at[which, b], w_recv.at[which, b], b, me_r).wait_recv()

    each(B - 1, w_arrived)
    for which in range(2):
        for b in range(B):
            w_all[which * B + b : which * B + b + 1, :] = rows_in[which, b].astype(F32)

    load.wait()
    pre = lax.dot_general(w_all[...].astype(BF16), tok[...], NT, preferred_element_type=F32)
    gate_pre, up_pre = pre[:B], pre[B:]
    s = jax.nn.sigmoid(gate_pre)
    active = gate_pre * s
    hidden = (active * up_pre).astype(BF16)

    def g_arrived(i):
        r = lax.rem(me_r + i + 1, R)

        def wait():
            remote(gram.at[r], gram.at[r], g_send.at[r], g_recv.at[r], me_b, r).wait_recv()

        if everyone:
            wait()
        else:
            pl.when(r < 2 * PX)(wait)

    each(R - 1, g_arrived)
    gd = gram[0]
    for r in range(1, 2 * PX):
        gd = gd + gram[r]
    hidden_grad = loss_scale * jnp.dot(
        gd[:, :B], hidden.astype(F32), precision=EXACT, preferred_element_type=F32
    )
    pair[pl.ds(0, B, stride=2), :] = hidden_grad * up_pre * (s * (1.0 + gate_pre * (1.0 - s)))
    pair[pl.ds(1, B, stride=2), :] = hidden_grad * active
    lhs = pair[...].astype(BF16)

    chunk = math.gcd(512, PW)

    def half(which, ref):
        for c in range(0, HW, chunk):
            col = pl.multiple_of(which * HW + c, 128)
            ref[:, c : c + chunk] = jnp.dot(lhs, tok[:, pl.ds(col, chunk)], preferred_element_type=F32)

    half(1 - core, part)
    part[:, HW:] = jnp.zeros((2 * B, 128), F32)
    part[0:B, HW : HW + B] = lax.dot_general(hidden, hidden, NT, preferred_element_type=F32)
    partner = remote(part, partner_in, p_send, p_recv, me_b, 2 * xi + 1 - core)
    partner.start()
    half(core, mine)
    partner.wait_recv()

    ghat = part[0:B, HW:] + partner_in[0:B, HW:]
    ghi = ghat.astype(BF16).astype(F32)
    glo = ghat - ghi
    for b in range(B):
        gpair = jnp.concatenate([ghi[b : b + 1], glo[b : b + 1]], axis=0).astype(BF16)
        for q in range(PX):
            cols = slice(q * PW, (q + 1) * PW)
            term = mine[2 * b : 2 * b + 2, cols] + partner_in[2 * b : 2 * b + 2, cols]
            send[b, q, :, 0:PW] = term.astype(BF16)
            send[b, q, :, PW:] = gpair

    def r_copy(i):
        b, r = same_core(i)
        q = lax.div(r, 2)
        at = me_b * XN + xi
        qq = q if everyone else lax.rem(q, PX)
        return q, remote(send.at[b, qq], recv.at[at], r_send.at[b * XN + q], r_recv.at[at], b, r)

    def for_r(act):
        def body(i):
            q, copy = r_copy(i)
            if everyone:
                act(copy)
            else:
                pl.when(q < PX)(lambda: act(copy))

        each(B * XN - 1, body)

    for_r(lambda copy: copy.start())

    def o_copy(i):
        r = lax.rem(me_r + i + 1, R)
        return remote(share.at[me_r], share.at[me_r], o_send.at[r], o_recv.at[me_r], me_b, r)

    def r_arrived(i):
        b, r = same_core(i)
        at = b * XN + lax.div(r, 2)
        remote(recv.at[at], recv.at[at], r_send.at[at], r_recv.at[at], b, r).wait_recv()

    def finish():
        recv[me_b * XN + xi] = send[me_b, xi if everyone else lax.rem(xi, PX)]
        each(B * XN - 1, r_arrived)
        n = B * XN
        if n <= 32:
            total = recv[0].astype(F32)
            for i in range(1, n):
                total = total + recv[i].astype(F32)
        else:
            total = lax.fori_loop(
                1, n, lambda i, c: c + recv[i].astype(F32), recv[0].astype(F32)
            )
        share[me_r, 0:2, :] = total[:, 0:PW]
        grow = total[0:1, PW:] + total[1:2, PW:]
        eye = lax.broadcasted_iota(jnp.int32, (B, 128), 0) == lax.broadcasted_iota(jnp.int32, (B, 128), 1)
        gcol = jnp.sum(jnp.where(eye, jnp.broadcast_to(grow, (B, 128)), 0.0), axis=1, keepdims=True)
        share[me_r, 2:3, :] = loss_scale * jnp.sum(gcol * wd_all[...], axis=0, keepdims=True)
        each(R - 1, lambda i: o_copy(i).start())

    if_owner(finish)

    def o_arrived(i):
        r = lax.rem(me_r + i + 1, R)

        def wait():
            remote(share.at[r], share.at[r], o_send.at[r], o_recv.at[r], me_b, r).wait_recv()

        if everyone:
            wait()
        else:
            pl.when(r < 2 * PX)(wait)

    each(R - 1, o_arrived)
    for r in range(2 * PX):
        col = (r % 2) * HW + (r // 2) * PW
        out_gate[:, col : col + PW] = share[r, 0:1, :]
        out_up[:, col : col + PW] = share[r, 1:2, :]
        out_down[:, col : col + PW] = share[r, 2:3, :]

    each(B - 1, lambda i: d_copy(i).wait_send())
    each(B - 1, lambda i: (w_copy(0, gate_ref, i).wait_send(), w_copy(1, up_ref, i).wait_send()))
    if_owner(lambda: each(R - 1, lambda i: g_copy(i).wait_send()))
    partner.wait_send()
    for_r(lambda copy: copy.wait_send())
    if_owner(lambda: each(R - 1, lambda i: o_copy(i).wait_send()))


def solution(mesh):
    B, R = mesh.shape["blk"], mesh.shape["rep"]
    XN = R // 2

    def per_device(tokens, gate_weight, up_weight, down_weight):
        T, F = tokens.shape
        HW = F // 2
        PX = math.gcd(XN, HW // 128)
        PW = HW // PX
        loss_scale = float(T * B * R) ** -0.5
        dma = pltpu.SemaphoreType.DMA
        vmem = pl.BlockSpec(memory_space=pltpu.VMEM)
        row = jax.ShapeDtypeStruct((1, F), F32)
        return pl.pallas_call(
            functools.partial(kernel, B, R, PX, loss_scale),
            out_shape=(row, row, row),
            in_specs=[pl.BlockSpec(memory_space=pl.ANY), vmem, vmem, vmem],
            out_specs=(vmem, vmem, vmem),
            scratch_shapes=[
                pltpu.VMEM((T, F), BF16),
                pltpu.VMEM((2, B, 1, F), BF16),
                pltpu.VMEM((B, 1, PW), BF16),
                pltpu.VMEM((2 * B, F), F32),
                pltpu.VMEM((B, PW), F32),
                pltpu.VMEM((R, B, 128), F32),
                pltpu.VMEM((2 * B, T), F32),
                pltpu.VMEM((2 * B, HW + 128), F32),
                pltpu.VMEM((2 * B, HW + 128), F32),
                pltpu.VMEM((2 * B, HW), F32),
                pltpu.VMEM((B, PX, 2, PW + 128), BF16),
                pltpu.VMEM((B * XN, 2, PW + 128), BF16),
                pltpu.VMEM((R, 3, PW), F32),
                dma, dma((2, B)), dma((2, B)), dma((B,)), dma((B,)), dma((R,)), dma((R,)),
                dma, dma, dma((B * XN,)), dma((B * XN,)), dma((R,)), dma((R,)),
            ],
            compiler_params=pltpu.CompilerParams(collective_id=0, has_side_effects=True),
        )(tokens, gate_weight, up_weight, down_weight)

    in_specs = (P(("blk", "rep"), None), P("blk", None), P("blk", None), P("blk", None))
    out_specs = (P("blk", None), P("blk", None), P("blk", None))
    return jax.shard_map(
        per_device, mesh=mesh, in_specs=in_specs, out_specs=out_specs, check_vma=False
    )
```

time: 225 us -> 39.1 us (0.17)
  waiting for transfers between devices: 107 us -> 0 us
  blocking collectives: 94.8 us -> 0 us
  Pallas kernels: 0 us -> 33.9 us
  between operations: 14.1 us -> 0.64 us
  matrix products: 3.94 us -> 0 us
    all_gather x3 -> x0, blocking collectives: 94.8 us -> none  [the longest x1 32.9 us: per_device(): down_piece = lax.all_gather(down_weight, 'blk', axis=0, tiled=True)]
    unnamed x3 -> x0, waiting for transfers between devices: 75.8 us -> none
    pallas_call x0 -> x1, Pallas kernels: none -> 33.9 us  [per_device(): pl.pallas_call(functools.partial(kernel, B, R, PX, loss_scale), out_shape...]
    psum x1 -> x0, waiting for transfers between devices: 31 us -> none  [per_device(): totals = lax.psum(shares, 'rep')]
    dot_general x7 -> x0, matrix products: 3.94 us -> none  [the longest x1 0.76 us: per_device(): jnp.dot(hidden_piece, down_piece, preferred_element_type=jnp.float32)]
  transfers between devices with their start and end apart: 2 -> 0, of which waited for: 2 -> 0; matrix products, arithmetic and copies ran while one was open for 0% -> 0% of each run, Pallas kernels for 0% -> 0%
where the time goes in v1:
time: 39.1 us; the launch traced here: 38.7 us
  Pallas kernels  33.9 us (87%)
  local copies, waits for them, and re-layouts  4.12 us (11%)
  between operations  0.64 us (2%)
    pallas_call x1, Pallas kernels, per_device(): pl.pallas_call(functools.partial(kernel, B, R, PX, loss_scale), out_shape...  33.9 us
    unnamed x3, local copies, waits for them, and re-layouts  4.12 us

profile of v1, /device:TPU:0, one launch (start us, length us, event | category | flops | bytes accessed | tf_op | source)
XLA Modules:
  0.0 38.7 jit_solution(10861793060073173705)
XLA Ops:
  0.6 33.9 %shard_map.67 = (f32[1,8192]{1,0:T(1,128)}, f32[1,8192]{1,0:T(1,128)}, f32[1,8192]{1,0:T(1,128)}) custom-call(bf16[128,8192]{1,0:T(8,128)(2,1)} %tok_hbm.1, bf16[1,8192]{1,0:T(2,128)(2,1)} %gate_ref.1, bf16[1,8192]{1,0:T(2,128)(2,1)} %up_ref.1, bf16[1,8192]{1,0:T(2,128)(2,1)} %down_ref.1), custom_call_target="tpu_custom_call" | custom-call | tf_op jit(solution)/shard_map/pallas_call | solution.py:262
  34.6 1.4 %copy.10 = f32[1,8192]{1,0:T(1,128)} copy(f32[1,8192]{1,0:T(1,128)} %get-tuple-element.6) | data formatting | bytes 65536
  35.9 1.4 %copy.11 = f32[1,8192]{1,0:T(1,128)} copy(f32[1,8192]{1,0:T(1,128)} %get-tuple-element.7) | data formatting | bytes 65536
  37.3 1.4 %copy.12 = f32[1,8192]{1,0:T(1,128)} copy(f32[1,8192]{1,0:T(1,128)} %get-tuple-element.8) | data formatting | bytes 65536

commit v2 on v1

--- a/solution.py
+++ b/solution.py
@@ -25,8 +25,9 @@
     B, R, PX, loss_scale,
     tok_hbm, gate_ref, up_ref, down_ref,
     out_gate, out_up, out_down,
-    tok, rows_in, down_in, w_all, wd_all, gram, pair, partner_in, part, mine, send, recv, share,
-    tok_sem, w_send, w_recv, d_send, d_recv, g_send, g_recv, p_send, p_recv, r_send, r_recv, o_send, o_recv,
+    tok, two, rows_in, down_in, w_all, wd_all, gram, pair, partner_in, part, send, recv, share,
+    tok_sem, w_send, w_recv, f_send, f_recv, d_send, d_recv, g_send, g_recv, p_send, p_recv,
+    r_send, r_recv, o_send, o_recv,
 ):
     T, F = tok.shape
     XN = R // 2
@@ -64,34 +65,49 @@
 
     each(B * XN - 1, lambda i: greet(*same_core(i)))
     each(XN, lambda i: greet(me_b, 2 * i + 1 - core))
+
+    my_col = pl.multiple_of(core * HW + lax.rem(xi, PX) * PW, 128)
+    other_core = 2 * xi + 1 - core
+    DW = PW // 2
+    two[0:1, :] = gate_ref[...].astype(F32)
+    two[1:2, :] = up_ref[...].astype(F32)
+    for h in range(2):
+        rows = two[:, h * HW : (h + 1) * HW]
+        rows_in[me_b, h] = rows.astype(BF16)
+        w_all[h, 0:2, :] = rows
+    for h in range(2):
+        cols = pl.ds(pl.multiple_of(my_col + h * DW, 128), DW)
+        two[h : h + 1, 0:DW] = down_ref[:, cols].astype(F32)
+    down_in[me_b] = two[:, 0:DW].astype(BF16)
+
     pl.semaphore_wait(barrier, B * XN - 1 + XN)
 
-    my_col = pl.multiple_of(core * HW + lax.rem(xi, PX) * PW, 128)
-
     def d_copy(i):
         b = lax.rem(me_b + i + 1, B)
-        return remote(
-            down_ref.at[:, pl.ds(my_col, PW)], down_in.at[me_b], d_send.at[b], d_recv.at[me_b], b, me_r
-        )
-
-    def w_copy(which, ref, i):
-        b = lax.rem(me_b + i + 1, B)
-        return remote(ref, rows_in.at[which, me_b], w_send.at[which, b], w_recv.at[which, me_b], b, me_r)
+        return remote(down_in.at[me_b], down_in.at[me_b], d_send.at[b], d_recv.at[me_b], b, me_r)
+
+    def w_copy(i):
+        b = lax.rem(me_b + i + 1, B)
+        slot = rows_in.at[me_b, core]
+        return remote(slot, slot, w_send.at[b], w_recv.at[me_b], b, me_r)
+
+    def f_copy(i):
+        b = lax.rem(me_b + i + 1, B)
+        slot = rows_in.at[b, core]
+        return remote(slot, slot, f_send.at[b], f_recv.at[b], me_b, other_core)
 
     each(B - 1, lambda i: d_copy(i).start())
-    each(B - 1, lambda i: (w_copy(0, gate_ref, i).start(), w_copy(1, up_ref, i).start()))
-
-    down_in[me_b] = down_ref[:, pl.ds(my_col, PW)]
-    rows_in[0, me_b] = gate_ref[...]
-    rows_in[1, me_b] = up_ref[...]
+    each(B - 1, lambda i: w_copy(i).start())
 
     def d_arrived(i):
         b = lax.rem(me_b + i + 1, B)
         remote(down_in.at[b], down_in.at[b], d_send.at[b], d_recv.at[b], b, me_r).wait_recv()
 
     each(B - 1, d_arrived)
-    for b in range(B):
-        wd_all[b : b + 1, :] = down_in[b].astype(F32)
+    for k in range(B):
+        for h in range(2):
+            rows = down_in[lax.rem(me_b + k, B)].astype(F32)
+            wd_all[k : k + 1, h * DW : (h + 1) * DW] = rows[h : h + 1]
 
     def g_copy(i):
         r = lax.rem(me_r + i + 1, R)
@@ -107,18 +123,27 @@
 
     def w_arrived(i):
         b = lax.rem(me_b + i + 1, B)
-        for which in range(2):
-            slot = rows_in.at[which, b]
-            remote(slot, slot, w_send.at[which, b], w_recv.at[which, b], b, me_r).wait_recv()
+        slot = rows_in.at[b, core]
+        remote(slot, slot, w_send.at[b], w_recv.at[b], b, me_r).wait_recv()
+        f_copy(i).start()
+        w_all[core, 2 * i + 2 : 2 * i + 4, :] = rows_in[b, core].astype(F32)
+
+    def f_arrived(i):
+        b = lax.rem(me_b + i + 1, B)
+        slot = rows_in.at[b, 1 - core]
+        remote(slot, slot, f_send.at[b], f_recv.at[b], me_b, other_core).wait_recv()
+        w_all[1 - core, 2 * i + 2 : 2 * i + 4, :] = rows_in[b, 1 - core].astype(F32)
+
+    def product(h):
+        cols = pl.ds(pl.multiple_of(h * HW, 128), HW)
+        return lax.dot_general(w_all[h].astype(BF16), tok[:, cols], NT, preferred_element_type=F32)
 
     each(B - 1, w_arrived)
-    for which in range(2):
-        for b in range(B):
-            w_all[which * B + b : which * B + b + 1, :] = rows_in[which, b].astype(F32)
-
     load.wait()
-    pre = lax.dot_general(w_all[...].astype(BF16), tok[...], NT, preferred_element_type=F32)
-    gate_pre, up_pre = pre[:B], pre[B:]
+    first = product(core)
+    each(B - 1, f_arrived)
+    pair[...] = first + product(1 - core)
+    gate_pre, up_pre = pair[pl.ds(0, B, stride=2), :], pair[pl.ds(1, B, stride=2), :]
     s = jax.nn.sigmoid(gate_pre)
     active = gate_pre * s
     hidden = (active * up_pre).astype(BF16)
@@ -147,48 +172,53 @@
 
     chunk = math.gcd(512, PW)
 
-    def half(which, ref):
-        for c in range(0, HW, chunk):
-            col = pl.multiple_of(which * HW + c, 128)
+    def terms(which, q, ref):
+        for c in range(0, PW, chunk):
+            col = pl.multiple_of(which * HW + q * PW + c, 128)
             ref[:, c : c + chunk] = jnp.dot(lhs, tok[:, pl.ds(col, chunk)], preferred_element_type=F32)
 
-    half(1 - core, part)
-    part[:, HW:] = jnp.zeros((2 * B, 128), F32)
-    part[0:B, HW : HW + B] = lax.dot_general(hidden, hidden, NT, preferred_element_type=F32)
-    partner = remote(part, partner_in, p_send, p_recv, me_b, 2 * xi + 1 - core)
-    partner.start()
-    half(core, mine)
-    partner.wait_recv()
-
-    ghat = part[0:B, HW:] + partner_in[0:B, HW:]
-    ghi = ghat.astype(BF16).astype(F32)
-    glo = ghat - ghi
-    for b in range(B):
-        gpair = jnp.concatenate([ghi[b : b + 1], glo[b : b + 1]], axis=0).astype(BF16)
-        for q in range(PX):
-            cols = slice(q * PW, (q + 1) * PW)
-            term = mine[2 * b : 2 * b + 2, cols] + partner_in[2 * b : 2 * b + 2, cols]
-            send[b, q, :, 0:PW] = term.astype(BF16)
-            send[b, q, :, PW:] = gpair
+    def p_copy(q):
+        return remote(part.at[q], partner_in.at[q], p_send.at[q], p_recv.at[q], me_b, other_core)
+
+    for q in range(PX):
+        terms(1 - core, q, part.at[q])
+        part[q, :, PW:] = jnp.zeros((2 * B, 128), F32)
+        if q == 0:
+            turn = lax.rem(lax.broadcasted_iota(jnp.int32, (B, B), 1) + me_b, B)
+            turn = turn == lax.broadcasted_iota(jnp.int32, (B, B), 0)
+            named = jnp.dot(turn.astype(F32).astype(BF16), hidden, preferred_element_type=F32).astype(BF16)
+            part[0, 0:B, PW : PW + B] = lax.dot_general(hidden, named, NT, preferred_element_type=F32)
+            own_g = part[0, 0:B, PW:]
+        p_copy(q).start()
 
     def r_copy(i):
         b, r = same_core(i)
         q = lax.div(r, 2)
         at = me_b * XN + xi
         qq = q if everyone else lax.rem(q, PX)
-        return q, remote(send.at[b, qq], recv.at[at], r_send.at[b * XN + q], r_recv.at[at], b, r)
-
-    def for_r(act):
+        return q, remote(send.at[lax.div(i + 1, XN), qq], recv.at[at], r_send.at[b * XN + q], r_recv.at[at], b, r)
+
+    def for_r(act, q_now):
         def body(i):
             q, copy = r_copy(i)
-            if everyone:
-                act(copy)
-            else:
-                pl.when(q < PX)(lambda: act(copy))
+            pl.when(q == q_now)(lambda: act(copy))
 
         each(B * XN - 1, body)
 
-    for_r(lambda copy: copy.start())
+    own = part.at[PX]
+    for q in range(PX):
+        terms(core, q, own)
+        p_copy(q).wait_recv()
+        if q == 0:
+            ghat = own_g + partner_in[0, 0:B, PW:]
+            ghi = ghat.astype(BF16).astype(F32)
+            glo = ghat - ghi
+        for b in range(B):
+            gpair = jnp.concatenate([ghi[b : b + 1], glo[b : b + 1]], axis=0).astype(BF16)
+            term = own[2 * b : 2 * b + 2, 0:PW] + partner_in[q, 2 * b : 2 * b + 2, 0:PW]
+            send[b, q, :, 0:PW] = term.astype(BF16)
+            send[b, q, :, PW:] = gpair
+        for_r(lambda copy: copy.start(), q)
 
     def o_copy(i):
         r = lax.rem(me_r + i + 1, R)
@@ -200,7 +230,7 @@
         remote(recv.at[at], recv.at[at], r_send.at[at], r_recv.at[at], b, r).wait_recv()
 
     def finish():
-        recv[me_b * XN + xi] = send[me_b, xi if everyone else lax.rem(xi, PX)]
+        recv[me_b * XN + xi] = send[0, xi if everyone else lax.rem(xi, PX)]
         each(B * XN - 1, r_arrived)
         n = B * XN
         if n <= 32:
@@ -213,7 +243,9 @@
             )
         share[me_r, 0:2, :] = total[:, 0:PW]
         grow = total[0:1, PW:] + total[1:2, PW:]
-        eye = lax.broadcasted_iota(jnp.int32, (B, 128), 0) == lax.broadcasted_iota(jnp.int32, (B, 128), 1)
+        eye = lax.rem(lax.broadcasted_iota(jnp.int32, (B, 128), 0) + me_b, B) == lax.broadcasted_iota(
+            jnp.int32, (B, 128), 1
+        )
         gcol = jnp.sum(jnp.where(eye, jnp.broadcast_to(grow, (B, 128)), 0.0), axis=1, keepdims=True)
         share[me_r, 2:3, :] = loss_scale * jnp.sum(gcol * wd_all[...], axis=0, keepdims=True)
         each(R - 1, lambda i: o_copy(i).start())
@@ -239,10 +271,11 @@
         out_down[:, col : col + PW] = share[r, 2:3, :]
 
     each(B - 1, lambda i: d_copy(i).wait_send())
-    each(B - 1, lambda i: (w_copy(0, gate_ref, i).wait_send(), w_copy(1, up_ref, i).wait_send()))
+    each(B - 1, lambda i: (w_copy(i).wait_send(), f_copy(i).wait_send()))
     if_owner(lambda: each(R - 1, lambda i: g_copy(i).wait_send()))
-    partner.wait_send()
-    for_r(lambda copy: copy.wait_send())
+    for q in range(PX):
+        p_copy(q).wait_send()
+        for_r(lambda copy: copy.wait_send(), q)
     if_owner(lambda: each(R - 1, lambda i: o_copy(i).wait_send()))
 
 
@@ -266,20 +299,20 @@
             out_specs=(vmem, vmem, vmem),
             scratch_shapes=[
                 pltpu.VMEM((T, F), BF16),
-                pltpu.VMEM((2, B, 1, F), BF16),
-                pltpu.VMEM((B, 1, PW), BF16),
-                pltpu.VMEM((2 * B, F), F32),
+                pltpu.VMEM((2, F), F32),
+                pltpu.VMEM((B, 2, 2, HW), BF16),
+                pltpu.VMEM((B, 2, PW // 2), BF16),
+                pltpu.VMEM((2, 2 * B, HW), F32),
                 pltpu.VMEM((B, PW), F32),
                 pltpu.VMEM((R, B, 128), F32),
                 pltpu.VMEM((2 * B, T), F32),
-                pltpu.VMEM((2 * B, HW + 128), F32),
-                pltpu.VMEM((2 * B, HW + 128), F32),
-                pltpu.VMEM((2 * B, HW), F32),
+                pltpu.VMEM((PX, 2 * B, PW + 128), F32),
+                pltpu.VMEM((PX + 1, 2 * B, PW + 128), F32),
                 pltpu.VMEM((B, PX, 2, PW + 128), BF16),
                 pltpu.VMEM((B * XN, 2, PW + 128), BF16),
                 pltpu.VMEM((R, 3, PW), F32),
-                dma, dma((2, B)), dma((2, B)), dma((B,)), dma((B,)), dma((R,)), dma((R,)),
-                dma, dma, dma((B * XN,)), dma((B * XN,)), dma((R,)), dma((R,)),
+                dma, dma((B,)), dma((B,)), dma((B,)), dma((B,)), dma((B,)), dma((B,)), dma((R,)), dma((R,)),
+                dma((PX,)), dma((PX,)), dma((B * XN,)), dma((B * XN,)), dma((R,)), dma((R,)),
             ],
             compiler_params=pltpu.CompilerParams(collective_id=0, has_side_effects=True),
         )(tokens, gate_weight, up_weight, down_weight)

time: 39.1 us -> 31.8 us (0.81)
  Pallas kernels: 33.9 us -> 26.7 us
    pallas_call x1, Pallas kernels: 33.9 us -> 26.7 us  [per_device(): pl.pallas_call(functools.partial(kernel, B, R, PX, loss_scale), out_shape...]
where the time goes in v2:
time: 31.8 us; the launch traced here: 31.4 us
  Pallas kernels  26.7 us (84%)
  local copies, waits for them, and re-layouts  4.12 us (13%)
  between operations  0.64 us (2%)
    pallas_call x1, Pallas kernels, per_device(): pl.pallas_call(functools.partial(kernel, B, R, PX, loss_scale), out_shape...  26.7 us
    unnamed x3, local copies, waits for them, and re-layouts  4.12 us

profile of v2, /device:TPU:0, one launch (start us, length us, event | category | flops | bytes accessed | tf_op | source)
XLA Modules:
  0.0 31.4 jit_solution(9445213967443091661)
XLA Ops:
  0.6 26.7 %shard_map.67 = (f32[1,8192]{1,0:T(1,128)}, f32[1,8192]{1,0:T(1,128)}, f32[1,8192]{1,0:T(1,128)}) custom-call(bf16[128,8192]{1,0:T(8,128)(2,1)} %tok_hbm.1, bf16[1,8192]{1,0:T(2,128)(2,1)} %gate_ref.1, bf16[1,8192]{1,0:T(2,128)(2,1)} %up_ref.1, bf16[1,8192]{1,0:T(2,128)(2,1)} %down_ref.1), custom_call_target="tpu_custom_call" | custom-call | tf_op jit(solution)/shard_map/pallas_call | solution.py:295
  27.3 1.4 %copy.10 = f32[1,8192]{1,0:T(1,128)} copy(f32[1,8192]{1,0:T(1,128)} %get-tuple-element.6) | data formatting | bytes 65536
  28.7 1.4 %copy.11 = f32[1,8192]{1,0:T(1,128)} copy(f32[1,8192]{1,0:T(1,128)} %get-tuple-element.7) | data formatting | bytes 65536
  30.1 1.4 %copy.12 = f32[1,8192]{1,0:T(1,128)} copy(f32[1,8192]{1,0:T(1,128)} %get-tuple-element.8) | data formatting | bytes 65536

commit v3 on v2

--- a/solution.py
+++ b/solution.py
@@ -23,10 +23,10 @@
 
 def kernel(
     B, R, PX, loss_scale,
-    tok_hbm, gate_ref, up_ref, down_ref,
-    out_gate, out_up, out_down,
-    tok, two, rows_in, down_in, w_all, wd_all, gram, pair, partner_in, part, send, recv, share,
-    tok_sem, w_send, w_recv, f_send, f_recv, d_send, d_recv, g_send, g_recv, p_send, p_recv,
+    tok_hbm, gate_hbm, up_hbm, down_hbm,
+    out,
+    tok, gate_ref, up_ref, down_ref, two, rows_in, down_in, w_all, wd_all, gram, pair, partner_in, part, send, recv, share,
+    tok_sem, in_sem, w_send, w_recv, f_send, f_recv, d_send, d_recv, g_send, g_recv, p_send, p_recv,
     r_send, r_recv, o_send, o_recv,
 ):
     T, F = tok.shape
@@ -49,9 +49,6 @@
             device_id={"blk": b, "rep": r}, device_id_type=pl.DeviceIdType.MESH,
         )
 
-    load = pltpu.make_async_copy(tok_hbm, tok, tok_sem)
-    load.start()
-
     barrier = pltpu.get_barrier_semaphore()
 
     def greet(b, r):
@@ -59,16 +56,31 @@
             barrier, inc=1, device_id={"blk": b, "rep": r}, device_id_type=pl.DeviceIdType.MESH
         )
 
+    def far(i):
+        upper = lax.div(me_b, (B + 1) // 2)
+        k = 1 + lax.rem(B - 2 - me_b + upper + (2 * upper - 1) * i + B - 1, B - 1)
+        return k, lax.rem(me_b + k, B)
+
     def same_core(i):
         k = i + 1
         return lax.rem(me_b + k // XN, B), 2 * lax.rem(xi + k % XN, XN) + core
 
-    each(B * XN - 1, lambda i: greet(*same_core(i)))
-    each(XN, lambda i: greet(me_b, 2 * i + 1 - core))
+    each(B - 1, lambda i: greet(far(i)[1], me_r))
+    each(R - 1, lambda i: greet(me_b, lax.rem(me_r + i + 1, R)))
+    own_rows = [
+        pltpu.make_async_copy(src, dst, in_sem.at[j])
+        for j, (src, dst) in enumerate(((gate_hbm, gate_ref), (up_hbm, up_ref), (down_hbm, down_ref)))
+    ]
+    for copy in own_rows:
+        copy.start()
+    load = pltpu.make_async_copy(tok_hbm, tok, tok_sem)
+    load.start()
 
     my_col = pl.multiple_of(core * HW + lax.rem(xi, PX) * PW, 128)
     other_core = 2 * xi + 1 - core
     DW = PW // 2
+    for copy in own_rows:
+        copy.wait()
     two[0:1, :] = gate_ref[...].astype(F32)
     two[1:2, :] = up_ref[...].astype(F32)
     for h in range(2):
@@ -80,14 +92,14 @@
         two[h : h + 1, 0:DW] = down_ref[:, cols].astype(F32)
     down_in[me_b] = two[:, 0:DW].astype(BF16)
 
-    pl.semaphore_wait(barrier, B * XN - 1 + XN)
+    pl.semaphore_wait(barrier, B - 1 + R - 1)
 
     def d_copy(i):
-        b = lax.rem(me_b + i + 1, B)
+        b = far(i)[1]
         return remote(down_in.at[me_b], down_in.at[me_b], d_send.at[b], d_recv.at[me_b], b, me_r)
 
     def w_copy(i):
-        b = lax.rem(me_b + i + 1, B)
+        b = far(i)[1]
         slot = rows_in.at[me_b, core]
         return remote(slot, slot, w_send.at[b], w_recv.at[me_b], b, me_r)
 
@@ -180,57 +192,65 @@
     def p_copy(q):
         return remote(part.at[q], partner_in.at[q], p_send.at[q], p_recv.at[q], me_b, other_core)
 
-    for q in range(PX):
-        terms(1 - core, q, part.at[q])
-        part[q, :, PW:] = jnp.zeros((2 * B, 128), F32)
-        if q == 0:
+    turns = [lax.rem(xi + 1 + j, PX) for j in range(PX)]
+    for j, q in enumerate(turns):
+        terms(1 - core, q, part.at[j])
+        part[j, :, PW:] = jnp.zeros((2 * B, 128), F32)
+        if j == 0:
             turn = lax.rem(lax.broadcasted_iota(jnp.int32, (B, B), 1) + me_b, B)
             turn = turn == lax.broadcasted_iota(jnp.int32, (B, B), 0)
             named = jnp.dot(turn.astype(F32).astype(BF16), hidden, preferred_element_type=F32).astype(BF16)
             part[0, 0:B, PW : PW + B] = lax.dot_general(hidden, named, NT, preferred_element_type=F32)
             own_g = part[0, 0:B, PW:]
-        p_copy(q).start()
-
-    def r_copy(i):
-        b, r = same_core(i)
-        q = lax.div(r, 2)
-        at = me_b * XN + xi
-        qq = q if everyone else lax.rem(q, PX)
-        return q, remote(send.at[lax.div(i + 1, XN), qq], recv.at[at], r_send.at[b * XN + q], r_recv.at[at], b, r)
-
-    def for_r(act, q_now):
-        def body(i):
-            q, copy = r_copy(i)
-            pl.when(q == q_now)(lambda: act(copy))
-
-        each(B * XN - 1, body)
+        p_copy(j).start()
+
+    at = me_b * XN + xi
+
+    def for_r(act, j):
+        q = turns[j]
+
+        def to(k, b):
+            act(
+                remote(
+                    send.at[j, k], recv.at[at], r_send.at[j, k], r_recv.at[at], b, 2 * q + core
+                )
+            )
+
+        each(B - 1, lambda i: to(*far(i)))
+        if not everyone:
+            pl.when(q != xi)(lambda: to(0, me_b))
+        elif j < PX - 1:
+            to(0, me_b)
 
     own = part.at[PX]
-    for q in range(PX):
+    for j, q in enumerate(turns):
         terms(core, q, own)
-        p_copy(q).wait_recv()
-        if q == 0:
+        p_copy(j).wait_recv()
+        if j == 0:
             ghat = own_g + partner_in[0, 0:B, PW:]
             ghi = ghat.astype(BF16).astype(F32)
             glo = ghat - ghi
         for b in range(B):
             gpair = jnp.concatenate([ghi[b : b + 1], glo[b : b + 1]], axis=0).astype(BF16)
-            term = own[2 * b : 2 * b + 2, 0:PW] + partner_in[q, 2 * b : 2 * b + 2, 0:PW]
-            send[b, q, :, 0:PW] = term.astype(BF16)
-            send[b, q, :, PW:] = gpair
-        for_r(lambda copy: copy.start(), q)
+            term = own[2 * b : 2 * b + 2, 0:PW] + partner_in[j, 2 * b : 2 * b + 2, 0:PW]
+            send[j, b, :, 0:PW] = term.astype(BF16)
+            send[j, b, :, PW:] = gpair
+        for_r(lambda copy: copy.start(), j)
+
+    def columns(r):
+        return out.at[:, :, pl.ds(pl.multiple_of(lax.rem(r, 2) * HW + lax.div(r, 2) * PW, 128), PW)]
 
     def o_copy(i):
-        r = lax.rem(me_r + i + 1, R)
-        return remote(share.at[me_r], share.at[me_r], o_send.at[r], o_recv.at[me_r], me_b, r)
+        r = lax.rem(me_r + 1 + lax.rem(i + 1, R - 1), R)
+        return remote(share, columns(me_r), o_send.at[r], o_recv.at[me_r], me_b, r)
 
     def r_arrived(i):
         b, r = same_core(i)
-        at = b * XN + lax.div(r, 2)
-        remote(recv.at[at], recv.at[at], r_send.at[at], r_recv.at[at], b, r).wait_recv()
+        n = b * XN + lax.div(r, 2)
+        remote(recv.at[n], recv.at[n], r_send.at[0, 0], r_recv.at[n], b, r).wait_recv()
 
     def finish():
-        recv[me_b * XN + xi] = send[0, xi if everyone else lax.rem(xi, PX)]
+        recv[at] = send[PX - 1, 0]
         each(B * XN - 1, r_arrived)
         n = B * XN
         if n <= 32:
@@ -241,14 +261,16 @@
             total = lax.fori_loop(
                 1, n, lambda i, c: c + recv[i].astype(F32), recv[0].astype(F32)
             )
-        share[me_r, 0:2, :] = total[:, 0:PW]
+        share[0] = total[0:1, 0:PW]
+        share[1] = total[1:2, 0:PW]
         grow = total[0:1, PW:] + total[1:2, PW:]
         eye = lax.rem(lax.broadcasted_iota(jnp.int32, (B, 128), 0) + me_b, B) == lax.broadcasted_iota(
             jnp.int32, (B, 128), 1
         )
         gcol = jnp.sum(jnp.where(eye, jnp.broadcast_to(grow, (B, 128)), 0.0), axis=1, keepdims=True)
-        share[me_r, 2:3, :] = loss_scale * jnp.sum(gcol * wd_all[...], axis=0, keepdims=True)
+        share[2] = loss_scale * jnp.sum(gcol * wd_all[...], axis=0, keepdims=True)
         each(R - 1, lambda i: o_copy(i).start())
+        pltpu.make_async_copy(share, columns(me_r), in_sem.at[0]).start()
 
     if_owner(finish)
 
@@ -256,7 +278,7 @@
         r = lax.rem(me_r + i + 1, R)
 
         def wait():
-            remote(share.at[r], share.at[r], o_send.at[r], o_recv.at[r], me_b, r).wait_recv()
+            remote(columns(r), columns(r), o_send.at[r], o_recv.at[r], me_b, r).wait_recv()
 
         if everyone:
             wait()
@@ -264,19 +286,18 @@
             pl.when(r < 2 * PX)(wait)
 
     each(R - 1, o_arrived)
-    for r in range(2 * PX):
-        col = (r % 2) * HW + (r // 2) * PW
-        out_gate[:, col : col + PW] = share[r, 0:1, :]
-        out_up[:, col : col + PW] = share[r, 1:2, :]
-        out_down[:, col : col + PW] = share[r, 2:3, :]
-
     each(B - 1, lambda i: d_copy(i).wait_send())
     each(B - 1, lambda i: (w_copy(i).wait_send(), f_copy(i).wait_send()))
     if_owner(lambda: each(R - 1, lambda i: g_copy(i).wait_send()))
-    for q in range(PX):
-        p_copy(q).wait_send()
-        for_r(lambda copy: copy.wait_send(), q)
-    if_owner(lambda: each(R - 1, lambda i: o_copy(i).wait_send()))
+    for j in range(PX):
+        p_copy(j).wait_send()
+        for_r(lambda copy: copy.wait_send(), j)
+
+    def left():
+        each(R - 1, lambda i: o_copy(i).wait_send())
+        pltpu.make_async_copy(share, columns(me_r), in_sem.at[0]).wait()
+
+    if_owner(left)
 
 
 def solution(mesh):
@@ -290,15 +311,18 @@
         PW = HW // PX
         loss_scale = float(T * B * R) ** -0.5
         dma = pltpu.SemaphoreType.DMA
-        vmem = pl.BlockSpec(memory_space=pltpu.VMEM)
-        row = jax.ShapeDtypeStruct((1, F), F32)
-        return pl.pallas_call(
+        hbm = pl.BlockSpec(memory_space=pl.ANY)
+
+        out = pl.pallas_call(
             functools.partial(kernel, B, R, PX, loss_scale),
-            out_shape=(row, row, row),
-            in_specs=[pl.BlockSpec(memory_space=pl.ANY), vmem, vmem, vmem],
-            out_specs=(vmem, vmem, vmem),
+            out_shape=jax.ShapeDtypeStruct((3, 1, F), F32),
+            in_specs=[hbm] * 4,
+            out_specs=hbm,
             scratch_shapes=[
                 pltpu.VMEM((T, F), BF16),
+                pltpu.VMEM((1, F), BF16),
+                pltpu.VMEM((1, F), BF16),
+                pltpu.VMEM((1, F), BF16),
                 pltpu.VMEM((2, F), F32),
                 pltpu.VMEM((B, 2, 2, HW), BF16),
                 pltpu.VMEM((B, 2, PW // 2), BF16),
@@ -308,14 +332,15 @@
                 pltpu.VMEM((2 * B, T), F32),
                 pltpu.VMEM((PX, 2 * B, PW + 128), F32),
                 pltpu.VMEM((PX + 1, 2 * B, PW + 128), F32),
-                pltpu.VMEM((B, PX, 2, PW + 128), BF16),
+                pltpu.VMEM((PX, B, 2, PW + 128), BF16),
                 pltpu.VMEM((B * XN, 2, PW + 128), BF16),
-                pltpu.VMEM((R, 3, PW), F32),
-                dma, dma((B,)), dma((B,)), dma((B,)), dma((B,)), dma((B,)), dma((B,)), dma((R,)), dma((R,)),
-                dma((PX,)), dma((PX,)), dma((B * XN,)), dma((B * XN,)), dma((R,)), dma((R,)),
+                pltpu.VMEM((3, 1, PW), F32),
+                dma, dma((3,)), dma((B,)), dma((B,)), dma((B,)), dma((B,)), dma((B,)), dma((B,)), dma((R,)), dma((R,)),
+                dma((PX,)), dma((PX,)), dma((PX, B)), dma((B * XN,)), dma((R,)), dma((R,)),
             ],
             compiler_params=pltpu.CompilerParams(collective_id=0, has_side_effects=True),
         )(tokens, gate_weight, up_weight, down_weight)
+        return out[0], out[1], out[2]
 
     in_specs = (P(("blk", "rep"), None), P("blk", None), P("blk", None), P("blk", None))
     out_specs = (P("blk", None), P("blk", None), P("blk", None))

time: 31.8 us -> 26.5 us (0.83)
  local copies, waits for them, and re-layouts: 4.12 us -> 1.43 us
  Pallas kernels: 26.7 us -> 24.2 us
    unnamed x3 -> x0, local copies, waits for them, and re-layouts: 4.12 us -> none
    pallas_call x1, Pallas kernels: 26.7 us -> 24.2 us  [per_device(): pl.pallas_call(functools.partial(kernel, B, R, PX, loss_scale), out_shape...]
    squeeze x0 -> x1, local copies, waits for them, and re-layouts: none -> 1.43 us  [per_device(): return (out[0], out[1], out[2])]
where the time goes in v3:
time: 26.5 us; the launch traced here: 26.3 us
  Pallas kernels  24.2 us (91%)
  local copies, waits for them, and re-layouts  1.43 us (5%)
  between operations  0.64 us (2%)
    pallas_call x1, Pallas kernels, per_device(): pl.pallas_call(functools.partial(kernel, B, R, PX, loss_scale), out_shape...  24.2 us
    squeeze x1, local copies, waits for them, and re-layouts, per_device(): return (out[0], out[1], out[2])  1.43 us

profile of v3, /device:TPU:0, one launch (start us, length us, event | category | flops | bytes accessed | tf_op | source)
XLA Modules:
  0.0 26.3 jit_solution(7933360389278649091)
XLA Ops:
  0.6 24.2 %shard_map.67 = f32[3,1,8192]{2,1,0:T(1,128)} custom-call(bf16[128,8192]{1,0:T(8,128)(2,1)} %tok_hbm.1, bf16[1,8192]{1,0:T(2,128)(2,1)} %gate_hbm.1, bf16[1,8192]{1,0:T(2,128)(2,1)} %up_hbm.1, bf16[1,8192]{1,0:T(2,128)(2,1)} %down_hbm.1), custom_call_target="tpu_custom_call" | custom-call | tf_op jit(solution)/shard_map/pallas_call | solution.py:316
  24.9 1.4 %slice_bitcast_fusion = (f32[1,8192]{1,0:T(1,128)}, f32[1,8192]{1,0:T(1,128)}, f32[1,8192]{1,0:T(1,128)}) fusion(f32[3,1,8192]{2,1,0:T(1,128)} %shard_map.67), kind=kLoop, calls=%fused_computation | loop fusion | bytes 196608 | tf_op jit(solution)/shard_map/squeeze | solution.py:343

commit v4 on v3

--- a/solution.py
+++ b/solution.py
@@ -315,9 +315,9 @@
 
         out = pl.pallas_call(
             functools.partial(kernel, B, R, PX, loss_scale),
-            out_shape=jax.ShapeDtypeStruct((3, 1, F), F32),
+            out_shape=pltpu.VMEM((3, 1, F), F32),
             in_specs=[hbm] * 4,
-            out_specs=hbm,
+            out_specs=pl.BlockSpec(memory_space=pltpu.VMEM),
             scratch_shapes=[
                 pltpu.VMEM((T, F), BF16),
                 pltpu.VMEM((1, F), BF16),

time: 26.5 us -> 25.5 us (0.962)
  local copies, waits for them, and re-layouts: 1.43 us -> 0.64 us
    squeeze x1, local copies, waits for them, and re-layouts: 1.43 us -> 0.64 us  [per_device(): return (out[0], out[1], out[2])]
where the time goes in v4:
time: 25.5 us; the launch traced here: 25.4 us
  Pallas kernels  24.1 us (95%)
  local copies, waits for them, and re-layouts  0.64 us (3%)
  between operations  0.64 us (3%)
    pallas_call x1, Pallas kernels, per_device(): pl.pallas_call(functools.partial(kernel, B, R, PX, loss_scale), out_shape...  24.1 us
    squeeze x1, local copies, waits for them, and re-layouts, per_device(): return (out[0], out[1], out[2])  0.64 us

profile of v4, /device:TPU:0, one launch (start us, length us, event | category | flops | bytes accessed | tf_op | source)
XLA Modules:
  0.0 25.4 jit_solution(381081626244935027)
XLA Ops:
  0.6 24.1 %shard_map.67 = f32[3,1,8192]{2,1,0:T(1,128)S(1)} custom-call(bf16[128,8192]{1,0:T(8,128)(2,1)} %tok_hbm.1, bf16[1,8192]{1,0:T(2,128)(2,1)} %gate_hbm.1, bf16[1,8192]{1,0:T(2,128)(2,1)} %up_hbm.1, bf16[1,8192]{1,0:T(2,128)(2,1)} %down_hbm.1), custom_call_target="tpu_custom_call" | custom-call | tf_op jit(solution)/shard_map/pallas_call | solution.py:316
  24.8 0.6 %slice_bitcast_fusion = (f32[1,8192]{1,0:T(1,128)}, f32[1,8192]{1,0:T(1,128)}, f32[1,8192]{1,0:T(1,128)}) fusion(f32[3,1,8192]{2,1,0:T(1,128)S(1)} %shard_map.67), kind=kLoop, calls=%fused_computation | loop fusion | bytes 196608 | tf_op jit(solution)/shard_map/squeeze | solution.py:343
